TPU v7x, 32 devices: a whole 2x2x4 slice. The times are simulated.
32 devices in a mesh: section: 8 (over z, y), tensor: 4 (over x, core).
Axes of the slice: x: 2, y: 2, z: 4, core: 2. Of those that a mesh axis runs over, the one named last changes fastest.
Arguments:
- inputs: bfloat16 [2, 163840], P(None, 'tensor'), may hold values from -6 to 6
- cotangent: bfloat16 [2, 163840], P(None, 'tensor'), may hold values from -6 to 6
- weights: bfloat16 [8, 2560, 10240], P('section', None, 'tensor'), may hold values from -0.0625 to 0.0625
- norm_gains: float32 [4, 2560], replicated, may hold values from 0.5 to 1.5
Outputs:
- layer_results: bfloat16 [8, 2, 163840], P('section', None, 'tensor')
All inputs are finite; a program needn't handle non-finite values.
Results may differ from a plain program's by a relative error of at most 0.02.
Values may be sent and summed in bfloat16 or wider, within the bound.
A program may use at most 64 MiB of HBM per device.

v0:
```python
import jax
import jax.numpy as jnp
from jax import lax
from jax.sharding import PartitionSpec as P

LAYERS = 4


epsilon = 1e-05


def swapped(block, axis, stride):
    count = lax.axis_size(axis)
    route = []
    for low in range(count):
        high = low | 1 << stride
        if high != low and high < count:
            route += [(low, high), (high, low)]
    return lax.ppermute(block, axis, route)


def passed_along(block, axis, distance):
    devices = range(lax.axis_size(axis))
    route = [(i - distance, i) for i in devices if i - distance in devices]
    return lax.ppermute(block, axis, route)


def gelu_tanh(values):
    return jax.nn.gelu(values, approximate=True)


def normalize(carried):
    widened = carried.astype(jnp.float32)
    inverse_rms = lax.rsqrt(jnp.mean(widened * widened, axis=-1, keepdims=True) + epsilon)
    return (widened * inverse_rms, inverse_rms)


def project_back(operand, weight):
    return lax.dot_general(
        operand, weight, (((1,), (1,)), ((), ())), preferred_element_type=jnp.float32
    )


def body(inputs, cotangent, weights, norm_gains):
    section_count = lax.axis_size("section")
    tensor_count = lax.axis_size("tensor")
    group_span = 2 * LAYERS
    stack_count = section_count // group_span
    stride = 2 * stack_count
    section_index = lax.axis_index("section")
    tensor_index = lax.axis_index("tensor")
    group_index = section_index % stride // 2
    layer_index = section_index // stride
    up_section = section_index % 2 == 0
    weight_block = weights[0]
    model_width = weight_block.shape[0]
    hidden_width = weight_block.shape[1]
    batch_count = inputs.shape[0] // stack_count
    piece_size = inputs.shape[1]
    row_count = piece_size * tensor_count // model_width
    share_rows = row_count // tensor_count
    own_inputs = lax.dynamic_slice_in_dim(inputs, group_index * batch_count, batch_count, 0)
    own_grads = lax.dynamic_slice_in_dim(cotangent, group_index * batch_count, batch_count, 0)
    full_inputs, full_grads = (
        lax.all_gather(own_inputs, "tensor", axis=1, tiled=True),
        lax.all_gather(own_grads, "tensor", axis=1, tiled=True),
    )
    gain_row = lax.dynamic_index_in_dim(
        norm_gains, group_index * LAYERS + layer_index, 0, keepdims=False
    )
    step_count = batch_count + 2 * LAYERS - 2
    first_layer = layer_index == 0
    last_layer = layer_index == LAYERS - 1

    def in_range(batch):
        return (batch >= 0) & (batch < batch_count)

    def slot_of(batch):
        return jnp.clip(batch, 0, batch_count - 1)

    def put_slot(table, value, slot, valid):
        old_value = lax.dynamic_index_in_dim(table, slot, 0, keepdims=False)
        return lax.dynamic_update_index_in_dim(table, jnp.where(valid, value, old_value), slot, 0)

    def advance(step_index, state_tuple):
        ahead_part, behind_part, stash_rows, parked, results = state_tuple
        ahead_held, behind_held = (
            lax.all_gather(ahead_part, "tensor", axis=0, tiled=True),
            lax.all_gather(behind_part, "tensor", axis=0, tiled=True),
        )
        fwd_batch = step_index - layer_index
        back_batch = step_index - 2 * (LAYERS - 1) + layer_index
        fwd_valid = in_range(fwd_batch)
        back_valid = in_range(back_batch)
        fwd_slot = slot_of(fwd_batch)
        back_slot = slot_of(back_batch)
        entry_block = lax.dynamic_index_in_dim(full_inputs, fwd_slot, 0, keepdims=False).reshape(
            row_count, model_width
        )
        fwd_rows = jnp.where(first_layer, entry_block, ahead_held)
        seed_block = lax.dynamic_index_in_dim(full_grads, back_slot, 0, keepdims=False).reshape(
            row_count, model_width
        )
        back_rows = jnp.where(last_layer, seed_block, behind_held)
        stash_rows = put_slot(stash_rows, fwd_rows, fwd_slot, fwd_valid & up_section)
        saved_rows = lax.dynamic_index_in_dim(stash_rows, back_slot, 0, keepdims=False)
        unit_fwd, _ = normalize(fwd_rows)
        unit_saved, inverse_saved = normalize(saved_rows)
        normed_fwd = (unit_fwd * gain_row).astype(jnp.bfloat16)
        normed_saved = (unit_saved * gain_row).astype(jnp.bfloat16)

        def up_work(operands):
            first_normed, second_normed, grad_rows = operands
            preact_both = jnp.dot(
                jnp.concatenate([first_normed, second_normed], axis=0),
                weight_block,
                preferred_element_type=jnp.float32,
            )
            return (
                gelu_tanh(preact_both[:row_count]).astype(jnp.bfloat16),
                preact_both[row_count:],
            )

        def down_work(operands):
            first_normed, second_normed, grad_rows = operands
            grad_hidden = jnp.dot(
                grad_rows, weight_block, preferred_element_type=jnp.float32
            ).astype(jnp.bfloat16)
            return (grad_hidden, jnp.zeros((row_count, hidden_width), jnp.float32))

        outgoing_hidden, preact_saved = lax.cond(
            up_section, up_work, down_work, (normed_fwd, normed_saved, back_rows)
        )
        incoming_hidden = swapped(outgoing_hidden, "section", 0)
        _, pullback = jax.vjp(gelu_tanh, preact_saved)
        grad_pre = pullback(incoming_hidden.astype(jnp.float32))[0].astype(jnp.bfloat16)
        operand = jnp.where(up_section, grad_pre, incoming_hidden)
        summed = lax.psum_scatter(
            project_back(operand, weight_block)
            .astype(jnp.bfloat16)
            .astype(jnp.float32)
            .astype(jnp.bfloat16),
            "tensor",
            scatter_dimension=0,
            tiled=True,
        ).astype(jnp.float32)
        row_start = tensor_index * share_rows
        fwd_part = lax.dynamic_slice_in_dim(fwd_rows, row_start, share_rows, 0)
        back_part = lax.dynamic_slice_in_dim(back_rows, row_start, share_rows, 0)
        unit_part = lax.dynamic_slice_in_dim(unit_saved, row_start, share_rows, 0)
        inverse_part = lax.dynamic_slice_in_dim(inverse_saved, row_start, share_rows, 0)
        grad_unit = summed * gain_row
        grad_input = inverse_part * (
            grad_unit - unit_part * jnp.mean(grad_unit * unit_part, axis=-1, keepdims=True)
        )
        grad_next = (back_part.astype(jnp.float32) + grad_input).astype(jnp.bfloat16)
        out_next = (fwd_part.astype(jnp.float32) + summed).astype(jnp.bfloat16)
        own_result = jnp.where(up_section, grad_next, out_next)
        partner_part = swapped(own_result, "section", 0)
        done_piece = own_result.reshape(-1)
        out_all = jnp.where(up_section, partner_part, out_next)
        grad_all = jnp.where(up_section, grad_next, partner_part)
        done_slot = jnp.where(up_section, back_slot, fwd_slot)
        done_valid = jnp.where(up_section, back_valid, fwd_valid)
        results = put_slot(results, done_piece, done_slot, done_valid)
        ahead_next = passed_along(out_all, "section", stride)
        behind_next = passed_along(grad_all, "section", -stride)
        return (ahead_next, behind_next, stash_rows, parked, results)

    initial = (
        jnp.zeros((share_rows, model_width), jnp.bfloat16),
        jnp.zeros((share_rows, model_width), jnp.bfloat16),
        jnp.zeros((batch_count, row_count, model_width), jnp.bfloat16),
        jnp.zeros((batch_count, piece_size), jnp.bfloat16),
        jnp.zeros((batch_count, piece_size), jnp.bfloat16),
    )
    finished = lax.fori_loop(0, step_count, advance, initial)
    return finished[4][None]


def solution(mesh):
    placed = (P(None, "tensor"), P(None, "tensor"), P("section", None, "tensor"), P())
    return jax.shard_map(
        body, mesh=mesh, in_specs=placed, out_specs=P("section", None, "tensor"), check_vma=False
    )
```

profile of v0, /device:TPU:0, one launch (start us, length us, event | category | flops | bytes accessed | tf_op | source)
XLA Modules:
  0.0 727.5 jit_solution(9746983331055812155)
XLA Ops:
  7.4 10.9 %all_gather.27 = bf16[2,163840]{1,0:T(2,128)(2,1)} all-gather(bf16[2,40960]{1,0:T(2,128)(2,1)} %param.8), channel_id=1, replica_groups=mesh['section'=8,'tensor'=4] {'tensor'}, dimensions={1}, use_global_device_ids=true | all-gather | bytes 819200 | tf_op jit(solution)/shard_map/all_gather | solution.py:65
  18.3 8.6 %all_gather.26 = bf16[2,163840]{1,0:T(2,128)(2,1)} all-gather(bf16[2,40960]{1,0:T(2,128)(2,1)} %param.9), channel_id=1, replica_groups=mesh['section'=8,'tensor'=4] {'tensor'}, dimensions={1}, use_global_device_ids=true | all-gather | bytes 819200 | tf_op jit(solution)/shard_map/all_gather | solution.py:66
  28.4 691.7 %while.21 = (s32[]{:T(128)}, bf16[16,2560]{1,0:T(8,128)(2,1)}, bf16[16,2560]{1,0:T(8,128)(2,1)}, bf16[2,64,2560]{2,1,0:T(8,128)(2,1)S(1)}, bf16[2,40960]{1,0:T(2...) while((s32[]{:T(128)}, bf16[16,2560]{1,0:T(8,128)(2,1)}, ...), condition=%wide.region_7.8_spmd, body=%wide.region_0.7_spmd.sunk | while | flops 2526863360 | bytes 47875124 | solution.py:177
  28.4 6.7 all_gather.30
  41.5 8.0 %dynamic-slice_reduce_fusion.4 = (bf16[163840]{0:T(1024)(128)(2,1)S(1)}, bf16[163840]{0:T(1024)(128)(2,1)S(1)}) fusion(bf16[2,163840]{1,0:T(2,128)(2,1)} %get-tuple-element.574, s32[]{:T(128)S(6)} %min.23, bf16[2,163840]{1,0:T(2,128)(2,1)} %get-tuple-element.571, s32[]{:T(128)S(6)} %min.24), kind=kLoop, calls=%fused_computation.30.clone.1 | loop fusion | bytes 1310728 | tf_op jit(solution)/shard_map/while/body/eval_jaxpr/jit(dynamic_index_in_dim)/dynamic_slice | solution.py:97
  51.1 7.0 conditional.3
  60.0 8.2 %collective-permute-done = bf16[64,2560]{1,0:T(8,128)(2,1)S(1)} collective-permute-done((bf16[64,2560]{1,0:T(8,128)(2,1)S(1)}, bf16[64,2560]{1,0:T(8,128)(2,1)S(1)}, u32[]{:S(2)}, u32[]{:S(2)}) %collective-permute-start) | collective-permute-done | bytes 327712 | tf_op jit(solution)/shard_map/while/body/eval_jaxpr/ppermute | solution.py:19
  68.3 9.5 %convolution_convert_fusion.2 = bf16[64,2560]{1,0:T(8,128)(2,1)} fusion(bf16[2560,2560]{1,0:T(8,128)(2,1)} %get-tuple-element.576, bf16[64,2560]{1,0:T(8,128)(2,1)S(1)} %collective-permute-done, f32[64,2560]{1,0:T(8,128)S(1)} %get-tuple-element.514, f32[64,2560]{1,0:T(8,128)S(1)} %get-tuple-element.515, pred[]{:T(512)} %get-tuple-element.568), kind=kOutput, calls=%fused_computation.13.clone.1 | convolution fusion | flops 842465280 | bytes 15073281 | tf_op jit(solution)/shard_map/while/body/eval_jaxpr/dot_general | solution.py:39
  77.9 21.9 %reduce-scatter.2.cloned.1.call-done = bf16[16,2560]{1,0:T(8,128)(2,1)} async-done(((bf16[64,2560]{1,0:T(8,128)(2,1)}), bf16[16,2560]{1,0:T(8,128)(2,1)}) %reduce-scatter.2.cloned.1.call-update) | async-done | bytes 81936 | tf_op jit(solution)/shard_map/while/body/eval_jaxpr/reduce_scatter | solution.py:138
  130.4 8.0 %dynamic-slice_reduce_fusion.4 = (bf16[163840]{0:T(1024)(128)(2,1)S(1)}, bf16[163840]{0:T(1024)(128)(2,1)S(1)}) fusion(bf16[2,163840]{1,0:T(2,128)(2,1)} %get-tuple-element.574, s32[]{:T(128)S(6)} %min.23, bf16[2,163840]{1,0:T(2,128)(2,1)} %get-tuple-element.571, s32[]{:T(128)S(6)} %min.24), kind=kLoop, calls=%fused_computation.30.clone.1 | loop fusion | bytes 1310728 | tf_op jit(solution)/shard_map/while/body/eval_jaxpr/jit(dynamic_index_in_dim)/dynamic_slice | solution.py:97
  139.9 7.0 conditional.3
  139.9 6.6 fusion.7
  148.7 8.3 %collective-permute-done = bf16[64,2560]{1,0:T(8,128)(2,1)S(1)} collective-permute-done((bf16[64,2560]{1,0:T(8,128)(2,1)S(1)}, bf16[64,2560]{1,0:T(8,128)(2,1)S(1)}, u32[]{:S(2)}, u32[]{:S(2)}) %collective-permute-start) | collective-permute-done | bytes 327712 | tf_op jit(solution)/shard_map/while/body/eval_jaxpr/ppermute | solution.py:19
  157.0 9.5 %convolution_convert_fusion.2 = bf16[64,2560]{1,0:T(8,128)(2,1)} fusion(bf16[2560,2560]{1,0:T(8,128)(2,1)} %get-tuple-element.576, bf16[64,2560]{1,0:T(8,128)(2,1)S(1)} %collective-permute-done, f32[64,2560]{1,0:T(8,128)S(1)} %get-tuple-element.514, f32[64,2560]{1,0:T(8,128)S(1)} %get-tuple-element.515, pred[]{:T(512)} %get-tuple-element.568), kind=kOutput, calls=%fused_computation.13.clone.1 | convolution fusion | flops 842465280 | bytes 15073281 | tf_op jit(solution)/shard_map/while/body/eval_jaxpr/dot_general | solution.py:39
  166.6 19.3 %reduce-scatter.2.cloned.1.call-done = bf16[16,2560]{1,0:T(8,128)(2,1)} async-done(((bf16[64,2560]{1,0:T(8,128)(2,1)}), bf16[16,2560]{1,0:T(8,128)(2,1)}) %reduce-scatter.2.cloned.1.call-update) | async-done | bytes 81936 | tf_op jit(solution)/shard_map/while/body/eval_jaxpr/reduce_scatter | solution.py:138
  216.4 8.0 %dynamic-slice_reduce_fusion.4 = (bf16[163840]{0:T(1024)(128)(2,1)S(1)}, bf16[163840]{0:T(1024)(128)(2,1)S(1)}) fusion(bf16[2,163840]{1,0:T(2,128)(2,1)} %get-tuple-element.574, s32[]{:T(128)S(6)} %min.23, bf16[2,163840]{1,0:T(2,128)(2,1)} %get-tuple-element.571, s32[]{:T(128)S(6)} %min.24), kind=kLoop, calls=%fused_computation.30.clone.1 | loop fusion | bytes 1310728 | tf_op jit(solution)/shard_map/while/body/eval_jaxpr/jit(dynamic_index_in_dim)/dynamic_slice | solution.py:97
  225.9 7.0 conditional.3
  234.7 8.3 %collective-permute-done = bf16[64,2560]{1,0:T(8,128)(2,1)S(1)} collective-permute-done((bf16[64,2560]{1,0:T(8,128)(2,1)S(1)}, bf16[64,2560]{1,0:T(8,128)(2,1)S(1)}, u32[]{:S(2)}, u32[]{:S(2)}) %collective-permute-start) | collective-permute-done | bytes 327712 | tf_op jit(solution)/shard_map/while/body/eval_jaxpr/ppermute | solution.py:19
  243.0 9.5 %convolution_convert_fusion.2 = bf16[64,2560]{1,0:T(8,128)(2,1)} fusion(bf16[2560,2560]{1,0:T(8,128)(2,1)} %get-tuple-element.576, bf16[64,2560]{1,0:T(8,128)(2,1)S(1)} %collective-permute-done, f32[64,2560]{1,0:T(8,128)S(1)} %get-tuple-element.514, f32[64,2560]{1,0:T(8,128)S(1)} %get-tuple-element.515, pred[]{:T(512)} %get-tuple-element.568), kind=kOutput, calls=%fused_computation.13.clone.1 | convolution fusion | flops 842465280 | bytes 15073281 | tf_op jit(solution)/shard_map/while/body/eval_jaxpr/dot_general | solution.py:39
  252.6 19.3 %reduce-scatter.2.cloned.1.call-done = bf16[16,2560]{1,0:T(8,128)(2,1)} async-done(((bf16[64,2560]{1,0:T(8,128)(2,1)}), bf16[16,2560]{1,0:T(8,128)(2,1)}) %reduce-scatter.2.cloned.1.call-update) | async-done | bytes 81936 | tf_op jit(solution)/shard_map/while/body/eval_jaxpr/reduce_scatter | solution.py:138
  302.4 8.0 %dynamic-slice_reduce_fusion.4 = (bf16[163840]{0:T(1024)(128)(2,1)S(1)}, bf16[163840]{0:T(1024)(128)(2,1)S(1)}) fusion(bf16[2,163840]{1,0:T(2,128)(2,1)} %get-tuple-element.574, s32[]{:T(128)S(6)} %min.23, bf16[2,163840]{1,0:T(2,128)(2,1)} %get-tuple-element.571, s32[]{:T(128)S(6)} %min.24), kind=kLoop, calls=%fused_computation.30.clone.1 | loop fusion | bytes 1310728 | tf_op jit(solution)/shard_map/while/body/eval_jaxpr/jit(dynamic_index_in_dim)/dynamic_slice | solution.py:97
  312.0 7.0 conditional.3
  312.0 6.6 fusion.7
  320.7 8.3 %collective-permute-done = bf16[64,2560]{1,0:T(8,128)(2,1)S(1)} collective-permute-done((bf16[64,2560]{1,0:T(8,128)(2,1)S(1)}, bf16[64,2560]{1,0:T(8,128)(2,1)S(1)}, u32[]{:S(2)}, u32[]{:S(2)}) %collective-permute-start) | collective-permute-done | bytes 327712 | tf_op jit(solution)/shard_map/while/body/eval_jaxpr/ppermute | solution.py:19
  329.0 9.5 %convolution_convert_fusion.2 = bf16[64,2560]{1,0:T(8,128)(2,1)} fusion(bf16[2560,2560]{1,0:T(8,128)(2,1)} %get-tuple-element.576, bf16[64,2560]{1,0:T(8,128)(2,1)S(1)} %collective-permute-done, f32[64,2560]{1,0:T(8,128)S(1)} %get-tuple-element.514, f32[64,2560]{1,0:T(8,128)S(1)} %get-tuple-element.515, pred[]{:T(512)} %get-tuple-element.568), kind=kOutput, calls=%fused_computation.13.clone.1 | convolution fusion | flops 842465280 | bytes 15073281 | tf_op jit(solution)/shard_map/while/body/eval_jaxpr/dot_general | solution.py:39
  338.6 19.3 %reduce-scatter.2.cloned.1.call-done = bf16[16,2560]{1,0:T(8,128)(2,1)} async-done(((bf16[64,2560]{1,0:T(8,128)(2,1)}), bf16[16,2560]{1,0:T(8,128)(2,1)}) %reduce-scatter.2.cloned.1.call-update) | async-done | bytes 81936 | tf_op jit(solution)/shard_map/while/body/eval_jaxpr/reduce_scatter | solution.py:138
  388.5 8.0 %dynamic-slice_reduce_fusion.4 = (bf16[163840]{0:T(1024)(128)(2,1)S(1)}, bf16[163840]{0:T(1024)(128)(2,1)S(1)}) fusion(bf16[2,163840]{1,0:T(2,128)(2,1)} %get-tuple-element.574, s32[]{:T(128)S(6)} %min.23, bf16[2,163840]{1,0:T(2,128)(2,1)} %get-tuple-element.571, s32[]{:T(128)S(6)} %min.24), kind=kLoop, calls=%fused_computation.30.clone.1 | loop fusion | bytes 1310728 | tf_op jit(solution)/shard_map/while/body/eval_jaxpr/jit(dynamic_index_in_dim)/dynamic_slice | solution.py:97
  398.0 7.0 conditional.3
  398.0 6.7 fusion.7
  406.8 8.3 %collective-permute-done = bf16[64,2560]{1,0:T(8,128)(2,1)S(1)} collective-permute-done((bf16[64,2560]{1,0:T(8,128)(2,1)S(1)}, bf16[64,2560]{1,0:T(8,128)(2,1)S(1)}, u32[]{:S(2)}, u32[]{:S(2)}) %collective-permute-start) | collective-permute-done | bytes 327712 | tf_op jit(solution)/shard_map/while/body/eval_jaxpr/ppermute | solution.py:19
  415.1 9.5 %convolution_convert_fusion.2 = bf16[64,2560]{1,0:T(8,128)(2,1)} fusion(bf16[2560,2560]{1,0:T(8,128)(2,1)} %get-tuple-element.576, bf16[64,2560]{1,0:T(8,128)(2,1)S(1)} %collective-permute-done, f32[64,2560]{1,0:T(8,128)S(1)} %get-tuple-element.514, f32[64,2560]{1,0:T(8,128)S(1)} %get-tuple-element.515, pred[]{:T(512)} %get-tuple-element.568), kind=kOutput, calls=%fused_computation.13.clone.1 | convolution fusion | flops 842465280 | bytes 15073281 | tf_op jit(solution)/shard_map/while/body/eval_jaxpr/dot_general | solution.py:39
  424.7 19.3 %reduce-scatter.2.cloned.1.call-done = bf16[16,2560]{1,0:T(8,128)(2,1)} async-done(((bf16[64,2560]{1,0:T(8,128)(2,1)}), bf16[16,2560]{1,0:T(8,128)(2,1)}) %reduce-scatter.2.cloned.1.call-update) | async-done | bytes 81936 | tf_op jit(solution)/shard_map/while/body/eval_jaxpr/reduce_scatter | solution.py:138
  474.5 8.0 %dynamic-slice_reduce_fusion.4 = (bf16[163840]{0:T(1024)(128)(2,1)S(1)}, bf16[163840]{0:T(1024)(128)(2,1)S(1)}) fusion(bf16[2,163840]{1,0:T(2,128)(2,1)} %get-tuple-element.574, s32[]{:T(128)S(6)} %min.23, bf16[2,163840]{1,0:T(2,128)(2,1)} %get-tuple-element.571, s32[]{:T(128)S(6)} %min.24), kind=kLoop, calls=%fused_computation.30.clone.1 | loop fusion | bytes 1310728 | tf_op jit(solution)/shard_map/while/body/eval_jaxpr/jit(dynamic_index_in_dim)/dynamic_slice | solution.py:97
  484.0 7.0 conditional.3
  492.8 8.3 %collective-permute-done = bf16[64,2560]{1,0:T(8,128)(2,1)S(1)} collective-permute-done((bf16[64,2560]{1,0:T(8,128)(2,1)S(1)}, bf16[64,2560]{1,0:T(8,128)(2,1)S(1)}, u32[]{:S(2)}, u32[]{:S(2)}) %collective-permute-start) | collective-permute-done | bytes 327712 | tf_op jit(solution)/shard_map/while/body/eval_jaxpr/ppermute | solution.py:19
  501.1 9.5 %convolution_convert_fusion.2 = bf16[64,2560]{1,0:T(8,128)(2,1)} fusion(bf16[2560,2560]{1,0:T(8,128)(2,1)} %get-tuple-element.576, bf16[64,2560]{1,0:T(8,128)(2,1)S(1)} %collective-permute-done, f32[64,2560]{1,0:T(8,128)S(1)} %get-tuple-element.514, f32[64,2560]{1,0:T(8,128)S(1)} %get-tuple-element.515, pred[]{:T(512)} %get-tuple-element.568), kind=kOutput, calls=%fused_computation.13.clone.1 | convolution fusion | flops 842465280 | bytes 15073281 | tf_op jit(solution)/shard_map/while/body/eval_jaxpr/dot_general | solution.py:39
  510.7 19.3 %reduce-scatter.2.cloned.1.call-done = bf16[16,2560]{1,0:T(8,128)(2,1)} async-done(((bf16[64,2560]{1,0:T(8,128)(2,1)}), bf16[16,2560]{1,0:T(8,128)(2,1)}) %reduce-scatter.2.cloned.1.call-update) | async-done | bytes 81936 | tf_op jit(solution)/shard_map/while/body/eval_jaxpr/reduce_scatter | solution.py:138
  560.5 8.0 %dynamic-slice_reduce_fusion.4 = (bf16[163840]{0:T(1024)(128)(2,1)S(1)}, bf16[163840]{0:T(1024)(128)(2,1)S(1)}) fusion(bf16[2,163840]{1,0:T(2,128)(2,1)} %get-tuple-element.574, s32[]{:T(128)S(6)} %min.23, bf16[2,163840]{1,0:T(2,128)(2,1)} %get-tuple-element.571, s32[]{:T(128)S(6)} %min.24), kind=kLoop, calls=%fused_computation.30.clone.1 | loop fusion | bytes 1310728 | tf_op jit(solution)/shard_map/while/body/eval_jaxpr/jit(dynamic_index_in_dim)/dynamic_slice | solution.py:97
  570.1 7.0 conditional.3
  578.8 8.3 %collective-permute-done = bf16[64,2560]{1,0:T(8,128)(2,1)S(1)} collective-permute-done((bf16[64,2560]{1,0:T(8,128)(2,1)S(1)}, bf16[64,2560]{1,0:T(8,128)(2,1)S(1)}, u32[]{:S(2)}, u32[]{:S(2)}) %collective-permute-start) | collective-permute-done | bytes 327712 | tf_op jit(solution)/shard_map/while/body/eval_jaxpr/ppermute | solution.py:19
  587.1 9.5 %convolution_convert_fusion.2 = bf16[64,2560]{1,0:T(8,128)(2,1)} fusion(bf16[2560,2560]{1,0:T(8,128)(2,1)} %get-tuple-element.576, bf16[64,2560]{1,0:T(8,128)(2,1)S(1)} %collective-permute-done, f32[64,2560]{1,0:T(8,128)S(1)} %get-tuple-element.514, f32[64,2560]{1,0:T(8,128)S(1)} %get-tuple-element.515, pred[]{:T(512)} %get-tuple-element.568), kind=kOutput, calls=%fused_computation.13.clone.1 | convolution fusion | flops 842465280 | bytes 15073281 | tf_op jit(solution)/shard_map/while/body/eval_jaxpr/dot_general | solution.py:39
  596.7 19.3 %reduce-scatter.2.cloned.1.call-done = bf16[16,2560]{1,0:T(8,128)(2,1)} async-done(((bf16[64,2560]{1,0:T(8,128)(2,1)}), bf16[16,2560]{1,0:T(8,128)(2,1)}) %reduce-scatter.2.cloned.1.call-update) | async-done | bytes 81936 | tf_op jit(solution)/shard_map/while/body/eval_jaxpr/reduce_scatter | solution.py:138
  646.6 8.0 %dynamic-slice_reduce_fusion.4 = (bf16[163840]{0:T(1024)(128)(2,1)S(1)}, bf16[163840]{0:T(1024)(128)(2,1)S(1)}) fusion(bf16[2,163840]{1,0:T(2,128)(2,1)} %get-tuple-element.574, s32[]{:T(128)S(6)} %min.23, bf16[2,163840]{1,0:T(2,128)(2,1)} %get-tuple-element.571, s32[]{:T(128)S(6)} %min.24), kind=kLoop, calls=%fused_computation.30.clone.1 | loop fusion | bytes 1310728 | tf_op jit(solution)/shard_map/while/body/eval_jaxpr/jit(dynamic_index_in_dim)/dynamic_slice | solution.py:97
  656.1 7.0 conditional.3
  656.2 6.7 fusion.7
  664.9 8.3 %collective-permute-done = bf16[64,2560]{1,0:T(8,128)(2,1)S(1)} collective-permute-done((bf16[64,2560]{1,0:T(8,128)(2,1)S(1)}, bf16[64,2560]{1,0:T(8,128)(2,1)S(1)}, u32[]{:S(2)}, u32[]{:S(2)}) %collective-permute-start) | collective-permute-done | bytes 327712 | tf_op jit(solution)/shard_map/while/body/eval_jaxpr/ppermute | solution.py:19
  673.2 9.5 %convolution_convert_fusion.2 = bf16[64,2560]{1,0:T(8,128)(2,1)} fusion(bf16[2560,2560]{1,0:T(8,128)(2,1)} %get-tuple-element.576, bf16[64,2560]{1,0:T(8,128)(2,1)S(1)} %collective-permute-done, f32[64,2560]{1,0:T(8,128)S(1)} %get-tuple-element.514, f32[64,2560]{1,0:T(8,128)S(1)} %get-tuple-element.515, pred[]{:T(512)} %get-tuple-element.568), kind=kOutput, calls=%fused_computation.13.clone.1 | convolution fusion | flops 842465280 | bytes 15073281 | tf_op jit(solution)/shard_map/while/body/eval_jaxpr/dot_general | solution.py:39
  682.8 19.3 %reduce-scatter.2.cloned.1.call-done = bf16[16,2560]{1,0:T(8,128)(2,1)} async-done(((bf16[64,2560]{1,0:T(8,128)(2,1)}), bf16[16,2560]{1,0:T(8,128)(2,1)}) %reduce-scatter.2.cloned.1.call-update) | async-done | bytes 81936 | tf_op jit(solution)/shard_map/while/body/eval_jaxpr/reduce_scatter | solution.py:138
  (260 shorter events, 296.9 us)
Async XLA Ops:
  6.5 0.8 copy-start
  28.4 71.4 %reduce-scatter.2.cloned.1.call-start = ((), (), s32[]{:S(2)}) async-start(), calls=%async_computation.1 | async-start | bytes 409600 | tf_op jit(solution)/shard_map/while/body/eval_jaxpr/reduce_scatter | solution.py:138
  58.1 10.1 %collective-permute-start = (bf16[64,2560]{1,0:T(8,128)(2,1)S(1)}, bf16[64,2560]{1,0:T(8,128)(2,1)S(1)}, u32[]{:S(2)}, u32[]{:S(2)}) collective-permute-start(bf16[64,2560]{1,0:T(8,128)(2,1)S(1)} %get-tuple-element.513), channel_id=1, source_target_pairs={{0,4},{4,0},{8,12},{12,8},{16,20},{20,16},{24,28},{28,24},{1,5},{5... | collective-permute-start | bytes 983048 | tf_op jit(solution)/shard_map/while/body/eval_jaxpr/ppermute | solution.py:19
  101.8 4.5 collective-permute-start.1
  107.3 7.2 collective-permute-start.2
  111.3 6.4 collective-permute-start.3
  117.8 68.1 %reduce-scatter.2.cloned.1.call-start = ((), (), s32[]{:S(2)}) async-start(), calls=%async_computation.1 | async-start | bytes 409600 | tf_op jit(solution)/shard_map/while/body/eval_jaxpr/reduce_scatter | solution.py:138
  146.9 10.0 %collective-permute-start = (bf16[64,2560]{1,0:T(8,128)(2,1)S(1)}, bf16[64,2560]{1,0:T(8,128)(2,1)S(1)}, u32[]{:S(2)}, u32[]{:S(2)}) collective-permute-start(bf16[64,2560]{1,0:T(8,128)(2,1)S(1)} %get-tuple-element.513), channel_id=1, source_target_pairs={{0,4},{4,0},{8,12},{12,8},{16,20},{20,16},{24,28},{28,24},{1,5},{5... | collective-permute-start | bytes 983048 | tf_op jit(solution)/shard_map/while/body/eval_jaxpr/ppermute | solution.py:19
  187.9 4.5 collective-permute-start.1
  193.3 7.2 collective-permute-start.2
  197.3 6.4 collective-permute-start.3
  203.8 68.1 %reduce-scatter.2.cloned.1.call-start = ((), (), s32[]{:S(2)}) async-start(), calls=%async_computation.1 | async-start | bytes 409600 | tf_op jit(solution)/shard_map/while/body/eval_jaxpr/reduce_scatter | solution.py:138
  232.9 10.0 %collective-permute-start = (bf16[64,2560]{1,0:T(8,128)(2,1)S(1)}, bf16[64,2560]{1,0:T(8,128)(2,1)S(1)}, u32[]{:S(2)}, u32[]{:S(2)}) collective-permute-start(bf16[64,2560]{1,0:T(8,128)(2,1)S(1)} %get-tuple-element.513), channel_id=1, source_target_pairs={{0,4},{4,0},{8,12},{12,8},{16,20},{20,16},{24,28},{28,24},{1,5},{5... | collective-permute-start | bytes 983048 | tf_op jit(solution)/shard_map/while/body/eval_jaxpr/ppermute | solution.py:19
  273.9 4.5 collective-permute-start.1
  279.4 7.2 collective-permute-start.2
  283.4 6.4 collective-permute-start.3
  289.8 68.1 %reduce-scatter.2.cloned.1.call-start = ((), (), s32[]{:S(2)}) async-start(), calls=%async_computation.1 | async-start | bytes 409600 | tf_op jit(solution)/shard_map/while/body/eval_jaxpr/reduce_scatter | solution.py:138
  319.0 10.0 %collective-permute-start = (bf16[64,2560]{1,0:T(8,128)(2,1)S(1)}, bf16[64,2560]{1,0:T(8,128)(2,1)S(1)}, u32[]{:S(2)}, u32[]{:S(2)}) collective-permute-start(bf16[64,2560]{1,0:T(8,128)(2,1)S(1)} %get-tuple-element.513), channel_id=1, source_target_pairs={{0,4},{4,0},{8,12},{12,8},{16,20},{20,16},{24,28},{28,24},{1,5},{5... | collective-permute-start | bytes 983048 | tf_op jit(solution)/shard_map/while/body/eval_jaxpr/ppermute | solution.py:19
  360.0 4.5 collective-permute-start.1
  365.4 7.2 collective-permute-start.2
  369.4 6.4 collective-permute-start.3
  375.9 68.1 %reduce-scatter.2.cloned.1.call-start = ((), (), s32[]{:S(2)}) async-start(), calls=%async_computation.1 | async-start | bytes 409600 | tf_op jit(solution)/shard_map/while/body/eval_jaxpr/reduce_scatter | solution.py:138
  405.0 10.0 %collective-permute-start = (bf16[64,2560]{1,0:T(8,128)(2,1)S(1)}, bf16[64,2560]{1,0:T(8,128)(2,1)S(1)}, u32[]{:S(2)}, u32[]{:S(2)}) collective-permute-start(bf16[64,2560]{1,0:T(8,128)(2,1)S(1)} %get-tuple-element.513), channel_id=1, source_target_pairs={{0,4},{4,0},{8,12},{12,8},{16,20},{20,16},{24,28},{28,24},{1,5},{5... | collective-permute-start | bytes 983048 | tf_op jit(solution)/shard_map/while/body/eval_jaxpr/ppermute | solution.py:19
  446.0 4.5 collective-permute-start.1
  451.4 7.2 collective-permute-start.2
  455.5 6.4 collective-permute-start.3
  461.9 68.1 %reduce-scatter.2.cloned.1.call-start = ((), (), s32[]{:S(2)}) async-start(), calls=%async_computation.1 | async-start | bytes 409600 | tf_op jit(solution)/shard_map/while/body/eval_jaxpr/reduce_scatter | solution.py:138
  491.1 10.0 %collective-permute-start = (bf16[64,2560]{1,0:T(8,128)(2,1)S(1)}, bf16[64,2560]{1,0:T(8,128)(2,1)S(1)}, u32[]{:S(2)}, u32[]{:S(2)}) collective-permute-start(bf16[64,2560]{1,0:T(8,128)(2,1)S(1)} %get-tuple-element.513), channel_id=1, source_target_pairs={{0,4},{4,0},{8,12},{12,8},{16,20},{20,16},{24,28},{28,24},{1,5},{5... | collective-permute-start | bytes 983048 | tf_op jit(solution)/shard_map/while/body/eval_jaxpr/ppermute | solution.py:19
  532.0 4.5 collective-permute-start.1
  537.5 7.2 collective-permute-start.2
  541.5 6.4 collective-permute-start.3
  547.9 68.1 %reduce-scatter.2.cloned.1.call-start = ((), (), s32[]{:S(2)}) async-start(), calls=%async_computation.1 | async-start | bytes 409600 | tf_op jit(solution)/shard_map/while/body/eval_jaxpr/reduce_scatter | solution.py:138
  577.1 10.0 %collective-permute-start = (bf16[64,2560]{1,0:T(8,128)(2,1)S(1)}, bf16[64,2560]{1,0:T(8,128)(2,1)S(1)}, u32[]{:S(2)}, u32[]{:S(2)}) collective-permute-start(bf16[64,2560]{1,0:T(8,128)(2,1)S(1)} %get-tuple-element.513), channel_id=1, source_target_pairs={{0,4},{4,0},{8,12},{12,8},{16,20},{20,16},{24,28},{28,24},{1,5},{5... | collective-permute-start | bytes 983048 | tf_op jit(solution)/shard_map/while/body/eval_jaxpr/ppermute | solution.py:19
  618.1 4.5 collective-permute-start.1
  623.5 7.2 collective-permute-start.2
  627.5 6.4 collective-permute-start.3
  634.0 68.1 %reduce-scatter.2.cloned.1.call-start = ((), (), s32[]{:S(2)}) async-start(), calls=%async_computation.1 | async-start | bytes 409600 | tf_op jit(solution)/shard_map/while/body/eval_jaxpr/reduce_scatter | solution.py:138
  663.2 10.0 %collective-permute-start = (bf16[64,2560]{1,0:T(8,128)(2,1)S(1)}, bf16[64,2560]{1,0:T(8,128)(2,1)S(1)}, u32[]{:S(2)}, u32[]{:S(2)}) collective-permute-start(bf16[64,2560]{1,0:T(8,128)(2,1)S(1)} %get-tuple-element.513), channel_id=1, source_target_pairs={{0,4},{4,0},{8,12},{12,8},{16,20},{20,16},{24,28},{28,24},{1,5},{5... | collective-permute-start | bytes 983048 | tf_op jit(solution)/shard_map/while/body/eval_jaxpr/ppermute | solution.py:19
  704.1 4.5 collective-permute-start.1
  709.5 7.2 collective-permute-start.2
  713.6 6.4 collective-permute-start.3
  720.0 0.7 copy-start.1
Sparse Core Ops, SparseCore 0:
  77.9 21.8 reduce-scatter.1
  166.6 19.1 reduce-scatter.1
  252.6 19.2 reduce-scatter.1
  338.7 19.2 reduce-scatter.1
  424.7 19.1 reduce-scatter.1
  510.7 19.2 reduce-scatter.1
  596.8 19.2 reduce-scatter.1
  682.8 19.1 reduce-scatter.1
where the time goes:
time: 730 us; the launch traced here: 728 us
  waiting for transfers between devices  272 us (37%)
  matrix products  129 us (18%)
  blocking collectives  121 us (17%)
  local copies, waits for them, and re-layouts  87.5 us (12%)
  starting transfers between devices  68.9 us (9%)
  other arithmetic  34.7 us (5%)
  between operations  13.4 us (2%)
    reduce_scatter x8, waiting for transfers between devices, advance(): lax.psum_scatter(project_back(operand, weight_block).astype(jnp.bfloat16)...  157 us
    ppermute x16, waiting for transfers between devices, swapped(): return lax.ppermute(block, axis, route)  88.9 us
    dot_general x8, matrix products, project_back(): lax.dot_general(operand, weight, (((1,), (1,)), ((), ())), preferred_elem...  76 us
    dynamic_slice x8, local copies, waits for them, and re-layouts, advance(): lax.dynamic_index_in_dim(full_inputs, fwd_slot, 0, keepdims=False)  63.9 us
    dot_general x8, matrix products, up_work(): jnp.dot(jnp.concatenate([first_normed, second_normed], axis=0), weight_bl...  53.2 us
    all_gather x8, blocking collectives, advance(): lax.all_gather(ahead_part, 'tensor', axis=0, tiled=True)  51.2 us
    all_gather x8, blocking collectives, advance(): lax.all_gather(behind_part, 'tensor', axis=0, tiled=True)  49.8 us
    ppermute x16, starting transfers between devices, passed_along(): return lax.ppermute(block, axis, route)  42.4 us
  transfers between devices with their start and end apart: 40, of which 32 were waited for; matrix products, arithmetic and copies ran while one was open for 2% of the time, Pallas kernels for 0%

commit v1 on v0

--- a/solution.py
+++ b/solution.py
@@ -1,8 +1,11 @@
+import functools
+
 import jax
 import jax.numpy as jnp
 from jax import lax
+from jax.experimental import pallas as pl
+from jax.experimental.pallas import tpu as pltpu
 from jax.sharding import PartitionSpec as P
-
 LAYERS = 4
 
 
@@ -41,7 +44,7 @@
     )
 
 
-def body(inputs, cotangent, weights, norm_gains):
+def plain_body(inputs, cotangent, weights, norm_gains):
     section_count = lax.axis_size("section")
     tensor_count = lax.axis_size("tensor")
     group_span = 2 * LAYERS
@@ -178,8 +181,374 @@
     return finished[4][None]
 
 
+MESH = pl.DeviceIdType.MESH
+ROW_TILE = 16
+GELU_C = 0.7978845608028654
+GELU_A = 0.044715
+PROJECT, COLLECT, FINISH = range(3)
+
+
+def orders(batches):
+    project = [PROJECT * batches + m for m in range(batches)]
+    back = []
+    for m in range(batches):
+        back += [COLLECT * batches + m, FINISH * batches + m]
+    turn = []
+    for m in range(batches):
+        turn += [PROJECT * batches + m]
+        if m:
+            turn += [FINISH * batches + m - 1]
+        turn += [COLLECT * batches + m]
+    turn += [FINISH * batches + batches - 1]
+    return project + back, turn, back + project, project + back
+
+
+def relay_kernel(
+    sections, tensors, stacks, batches,
+    x_ref, g_ref, w_hbm, gain_ref, out_ref,
+    w, gathered, resid, normed, hid_out, hid_in, slope, operand, total,
+    part_out, part_in, done,
+    w_sem, hid_send, hid_recv, part_send, part_recv, row_send, row_recv, res_send, res_recv,
+):
+    stride = 2 * stacks
+    share, width = x_ref.shape[1], x_ref.shape[2]
+    chunks, _, piece = w.shape
+    rows = tensors * share
+    s = lax.axis_index("section")
+    t = lax.axis_index("tensor")
+    layer = s // stride
+    stack = (s % stride) // 2
+    is_down = s % 2
+    is_up = is_down == 0
+    first = layer == 0
+    last = layer == LAYERS - 1
+    peer = s + 1 - 2 * is_down
+    along = s + stride * (2 * is_down - 1)
+    behind = s - stride * (2 * is_down - 1)
+    target = along + 1 - 2 * is_down
+    entry = (is_up & first) | (~is_up & last)
+    opening = (is_up & last) | (~is_up & first)
+    has_next = ~entry
+    has_prev = ~opening
+
+    def weight_copy(c):
+        return pltpu.make_async_copy(
+            w_hbm.at[:, pl.ds(pl.multiple_of(c * piece, piece), piece)], w.at[c], w_sem.at[c]
+        )
+
+    def other(d):
+        return lax.rem(t + d, tensors)
+
+    def hid_copy(m, c):
+        return pltpu.make_async_remote_copy(
+            hid_out.at[m, c], hid_in.at[m, c], hid_send.at[m, c], hid_recv.at[m, c],
+            device_id=(peer, t), device_id_type=MESH,
+        )
+
+    def part_copy(m, j):
+        return pltpu.make_async_remote_copy(
+            part_out.at[m, j], part_in.at[m, t], part_send.at[m, j], part_recv.at[m, t],
+            device_id=(s, j), device_id_type=MESH,
+        )
+
+    def row_copy(m, j, section):
+        return pltpu.make_async_remote_copy(
+            done.at[m], gathered.at[m, t], row_send.at[m, j], row_recv.at[m, t],
+            device_id=(section, j), device_id_type=MESH,
+        )
+
+    def res_copy(m):
+        return pltpu.make_async_remote_copy(
+            done.at[m], resid.at[m], res_send.at[m], res_recv.at[m],
+            device_id=(along, t), device_id_type=MESH,
+        )
+
+    def start_weight(c, carry):
+        weight_copy(c).start()
+        return carry
+
+    lax.fori_loop(0, chunks, start_weight, 0)
+
+    barrier = pltpu.get_barrier_semaphore()
+
+    def greet(section, j):
+        pl.semaphore_signal(barrier, inc=1, device_id=(section, j), device_id_type=MESH)
+
+    greet(peer, t)
+    for d in range(1, tensors):
+        greet(s, other(d))
+
+    @pl.when(has_next)
+    def _():
+        greet(along, t)
+        for d in range(tensors):
+            greet(target, other(d))
+
+    @pl.when(has_prev)
+    def _():
+        greet(behind, t)
+
+    next_count = jnp.where(has_next, tensors + 1, 0)
+    prev_count = jnp.where(has_prev, 1, 0)
+    pl.semaphore_wait(barrier, tensors + next_count + prev_count)
+
+    for m in range(batches):
+        at = stack * batches + m
+
+        @pl.when(is_up & first)
+        def _():
+            done[m] = x_ref[at]
+
+        @pl.when(~is_up & last)
+        def _():
+            done[m] = g_ref[at]
+
+        @pl.when(is_up & last)
+        def _():
+            resid[m] = g_ref[at]
+
+        @pl.when(~is_up & first)
+        def _():
+            resid[m] = x_ref[at]
+
+        @pl.when(entry)
+        def _():
+            for d in range(1, tensors):
+                row_copy(m, other(d), s).start()
+            gathered[m, t] = done[m]
+
+    gain = gain_ref[pl.ds(stack * LAYERS + layer, 1), :]
+    sequences = orders(batches)
+
+    def project(step, m):
+        for d in range(1, tensors):
+            j = other(d)
+            pltpu.make_async_copy(gathered.at[m, j], gathered.at[m, j], row_recv.at[m, j]).wait()
+
+        @pl.when(has_prev_rows)
+        def _():
+            pltpu.make_async_copy(gathered.at[m, t], gathered.at[m, t], row_recv.at[m, t]).wait()
+
+        @pl.when(is_up)
+        def _():
+            for j in range(tensors):
+                unit, _ = normalize(gathered[m, j])
+                normed[j * share:(j + 1) * share, :] = (unit * gain).astype(jnp.bfloat16)
+
+        @pl.when(~is_up)
+        def _():
+            for j in range(tensors):
+                normed[j * share:(j + 1) * share, :] = gathered[m, j]
+
+        def one(c, carry):
+            @pl.when(step == 0)
+            def _():
+                weight_copy(c).wait()
+
+            value = jnp.dot(normed[...], w[c], preferred_element_type=jnp.float32)
+
+            @pl.when(is_up)
+            def _():
+                square = value * value
+                tanh = jnp.tanh(GELU_C * value * (1.0 + GELU_A * square))
+                half = 0.5 * (1.0 + tanh)
+                hid_out[m, c] = (value * half).astype(jnp.bfloat16)
+                slope[m, c] = half + 0.5 * value * (1.0 - tanh * tanh) * (
+                    GELU_C * (1.0 + 3.0 * GELU_A * square)
+                )
+
+            @pl.when(~is_up)
+            def _():
+                hid_out[m, c] = value.astype(jnp.bfloat16)
+
+            hid_copy(m, c).start()
+            return carry
+
+        lax.fori_loop(0, chunks, one, 0)
+
+    def collect(step, m):
+        total[...] = jnp.zeros_like(total)
+
+        def one(c, carry):
+            @pl.when(step == 0)
+            def _():
+                weight_copy(c).wait()
+
+            hid_copy(m, c).wait_recv()
+
+            @pl.when(is_up)
+            def _():
+                operand[...] = (hid_in[m, c].astype(jnp.float32) * slope[m, c]).astype(jnp.bfloat16)
+
+            @pl.when(~is_up)
+            def _():
+                operand[...] = hid_in[m, c]
+
+            for n in range(width // piece):
+                cut = slice(n * piece, (n + 1) * piece)
+                total[:, cut] += project_back(operand[...], w[c, cut, :])
+            return carry
+
+        lax.fori_loop(0, chunks, one, 0)
+        for j in range(tensors):
+            part_out[m, j] = total[j * share:(j + 1) * share, :].astype(jnp.bfloat16)
+        for d in range(1, tensors):
+            part_copy(m, other(d)).start()
+
+    def finish(m):
+        for d in range(1, tensors):
+            j = other(d)
+            pltpu.make_async_copy(part_in.at[m, j], part_in.at[m, j], part_recv.at[m, j]).wait()
+
+        summed = part_out[m, t].astype(jnp.float32)
+        for d in range(1, tensors):
+            summed = summed + part_in[m, other(d)].astype(jnp.float32)
+
+        @pl.when(has_prev)
+        def _():
+            pltpu.make_async_copy(resid.at[m], resid.at[m], res_recv.at[m]).wait()
+
+        @pl.when(is_up)
+        def _():
+            unit, inverse = normalize(gathered[m, t])
+            grad = summed * gain
+            delta = inverse * (grad - unit * jnp.mean(grad * unit, axis=-1, keepdims=True))
+            value = (resid[m].astype(jnp.float32) + delta).astype(jnp.bfloat16)
+            out_ref[m] = value
+
+        @pl.when(~is_up)
+        def _():
+            out_ref[m] = (resid[m].astype(jnp.float32) + summed).astype(jnp.bfloat16)
+
+        @pl.when(has_next)
+        def _():
+            done[m] = out_ref[m]
+            for d in range(tensors):
+                row_copy(m, other(d), target).start()
+            res_copy(m).start()
+
+    has_prev_rows = ~entry
+
+    def advance(step, carry):
+        code = 0
+        for i in range(3 * batches):
+            steady_up, last_up, steady_down, last_down = (table[i] for table in sequences)
+            chosen = jnp.where(
+                is_up,
+                jnp.where(last, last_up, steady_up),
+                jnp.where(last, last_down, steady_down),
+            )
+            code = jnp.where(step == i, chosen, code)
+        kind, m = code // batches, code % batches
+
+        @pl.when(kind == PROJECT)
+        def _():
+            project(step, m)
+
+        @pl.when(kind == COLLECT)
+        def _():
+            collect(step, m)
+
+        @pl.when(kind == FINISH)
+        def _():
+            finish(m)
+
+        return carry
+
+    lax.fori_loop(0, 3 * batches, advance, 0)
+
+    def drain(m, carry):
+        def drain_hidden(c, inner):
+            hid_copy(m, c).wait_send()
+            return inner
+
+        lax.fori_loop(0, chunks, drain_hidden, 0)
+        for d in range(1, tensors):
+            part_copy(m, other(d)).wait_send()
+
+        for d in range(1, tensors):
+            row_copy(m, other(d), s).wait_send()
+
+        @pl.when(has_next)
+        def _():
+            row_copy(m, t, target).wait_send()
+            res_copy(m).wait_send()
+
+        return carry
+
+    lax.fori_loop(0, batches, drain, 0)
+
+
+def relay_body(mesh_shape, inputs, cotangent, weights, norm_gains):
+    sections, tensors = mesh_shape["section"], mesh_shape["tensor"]
+    stacks = sections // (2 * LAYERS)
+    width, hidden = weights.shape[1], weights.shape[2]
+    batches = inputs.shape[0] // stacks
+    share = inputs.shape[1] // width
+    rows = share * tensors
+    piece = chunk_of(width, hidden)
+    chunks = hidden // piece
+    bf16, f32 = jnp.bfloat16, jnp.float32
+    dma = pltpu.SemaphoreType.DMA
+    vmem = pl.BlockSpec(memory_space=pltpu.VMEM)
+    out = pl.pallas_call(
+        functools.partial(relay_kernel, sections, tensors, stacks, batches),
+        out_shape=jax.ShapeDtypeStruct((batches, share, width), bf16),
+        in_specs=[vmem, vmem, pl.BlockSpec(memory_space=pl.ANY), vmem],
+        out_specs=vmem,
+        scratch_shapes=[
+            pltpu.VMEM((chunks, width, piece), bf16),
+            pltpu.VMEM((batches, tensors, share, width), bf16),
+            pltpu.VMEM((batches, share, width), bf16),
+            pltpu.VMEM((rows, width), bf16),
+            pltpu.VMEM((batches, chunks, rows, piece), bf16),
+            pltpu.VMEM((batches, chunks, rows, piece), bf16),
+            pltpu.VMEM((batches, chunks, rows, piece), f32),
+            pltpu.VMEM((rows, piece), bf16),
+            pltpu.VMEM((rows, width), f32),
+            pltpu.VMEM((batches, tensors, share, width), bf16),
+            pltpu.VMEM((batches, tensors, share, width), bf16),
+            pltpu.VMEM((batches, share, width), bf16),
+            dma((chunks,)),
+            dma((batches, chunks)),
+            dma((batches, chunks)),
+            dma((batches, tensors)),
+            dma((batches, tensors)),
+            dma((batches, tensors)),
+            dma((batches, tensors)),
+            dma((batches,)),
+            dma((batches,)),
+        ],
+        compiler_params=pltpu.CompilerParams(
+            collective_id=0, has_side_effects=True, vmem_limit_bytes=67043328
+        ),
+    )(
+        inputs.reshape(-1, share, width),
+        cotangent.reshape(-1, share, width),
+        weights[0],
+        norm_gains,
+    )
+    return out.reshape(1, batches, share * width)
+
+
+def chunk_of(width, hidden):
+    for piece in (512, 256, 128):
+        if width % piece == 0 and hidden % piece == 0:
+            return piece
+    return 0
+
+
 def solution(mesh):
     placed = (P(None, "tensor"), P(None, "tensor"), P("section", None, "tensor"), P())
-    return jax.shard_map(
-        body, mesh=mesh, in_specs=placed, out_specs=P("section", None, "tensor"), check_vma=False
-    )
+
+    def run(inputs, cotangent, weights, norm_gains):
+        tensors = mesh.shape["tensor"]
+        width, hidden = weights.shape[1], weights.shape[2] // tensors
+        local = inputs.shape[1] // tensors
+        aligned = local % (ROW_TILE * width) == 0 and chunk_of(width, hidden)
+        body = functools.partial(relay_body, dict(mesh.shape)) if aligned else plain_body
+        return jax.shard_map(
+            body, mesh=mesh, in_specs=placed, out_specs=P("section", None, "tensor"), check_vma=False
+        )(inputs, cotangent, weights, norm_gains)
+
+    return run

time: 730 us -> 188 us (0.26)
  waiting for transfers between devices: 272 us -> 0 us
  Pallas kernels: 0 us -> 184 us
  matrix products: 129 us -> 0 us
  blocking collectives: 121 us -> 0 us
  local copies, waits for them, and re-layouts: 87.5 us -> 3.44 us
  starting transfers between devices: 68.9 us -> 0 us
  other arithmetic: 34.7 us -> 0 us
  between operations: 13.4 us -> 0.01 us
    pallas_call x0 -> x1, Pallas kernels: none -> 184 us  [relay_body(): pl.pallas_call(functools.partial(relay_kernel, sections, tensors, stacks,...]
    reduce_scatter x8 -> x0, waiting for transfers between devices: 157 us -> none  [advance(): lax.psum_scatter(project_back(operand, weight_block).astype(jnp.bfloat16)...]
    dot_general x16 -> x0, matrix products: 129 us -> none  [the longest x8 76 us: project_back(): lax.dot_general(operand, weight, (((1,), (1,)), ((), ())), preferred_elem...]
    all_gather x18 -> x0, blocking collectives: 121 us -> none  [the longest x8 51.2 us: advance(): lax.all_gather(ahead_part, 'tensor', axis=0, tiled=True)]
    ppermute x32 -> x0, waiting for transfers between devices: 115 us -> none  [the longest x16 88.9 us: swapped(): return lax.ppermute(block, axis, route)]
    ppermute x32 -> x0, starting transfers between devices: 68.8 us -> none  [the longest x16 42.4 us: passed_along(): return lax.ppermute(block, axis, route)]
    dynamic_slice x17 -> x0, local copies, waits for them, and re-layouts: 64.1 us -> none  [the longest x8 63.9 us: advance(): lax.dynamic_index_in_dim(full_inputs, fwd_slot, 0, keepdims=False)]
    select_n x32 -> x0, other arithmetic: 17.9 us -> none  [the longest x8 8.02 us: advance(): own_result = jnp.where(up_section, grad_next, out_next)]
  transfers between devices with their start and end apart: 40 -> 0, of which waited for: 32 -> 0; matrix products, arithmetic and copies ran while one was open for 2% -> 0% of each run, Pallas kernels for 0% -> 0%
where the time goes in v1:
time: 188 us
  Pallas kernels  184 us (98%)
  local copies, waits for them, and re-layouts  3.44 us (2%)
    pallas_call x1, Pallas kernels, relay_body(): pl.pallas_call(functools.partial(relay_kernel, sections, tensors, stacks,...  184 us

profile of v1, /device:TPU:0, one launch (start us, length us, event | category | flops | bytes accessed | tf_op | source)
XLA Modules:
  0.0 187.8 jit_solution(7769090325865465966)
XLA Ops:
  0.0 1.7 copy_bitcast_fusion
  1.7 184.3 %shard_map.46 = bf16[2,16,2560]{2,1,0:T(8,128)(2,1)} custom-call(bf16[2,16,2560]{2,1,0:T(8,128)(2,1)} %get-tuple-element.6.x_ref, bf16[2,16,2560]{2,1,0:T(8,128)(2,1)} %get-tuple-element.5.g_ref, bf16[2560,2560]{1,0:T(8,128)(2,1)} %bitcast.7, f32[4,2560]{1,0:T(4,128)} %gain_ref.1), custom_call_target="tpu_custom_call" | custom-call | tf_op jit(solution)/shard_map/pallas_call | solution.py:494
  186.1 1.7 reshape.11

commit v2 on v1

--- a/solution.py
+++ b/solution.py
@@ -182,7 +182,7 @@
 
 
 MESH = pl.DeviceIdType.MESH
-ROW_TILE = 16
+ROW_TILE = 8
 GELU_C = 0.7978845608028654
 GELU_A = 0.044715
 PROJECT, COLLECT, FINISH = range(3)
@@ -190,15 +190,14 @@
 
 def orders(batches):
     project = [PROJECT * batches + m for m in range(batches)]
-    back = []
-    for m in range(batches):
-        back += [COLLECT * batches + m, FINISH * batches + m]
-    turn = []
+    back, turn = [], []
     for m in range(batches):
         turn += [PROJECT * batches + m]
-        if m:
-            turn += [FINISH * batches + m - 1]
-        turn += [COLLECT * batches + m]
+        for order in (back, turn):
+            order += [COLLECT * batches + m]
+            if m:
+                order += [FINISH * batches + m - 1]
+    back += [FINISH * batches + batches - 1]
     turn += [FINISH * batches + batches - 1]
     return project + back, turn, back + project, project + back
 
@@ -208,7 +207,7 @@
     x_ref, g_ref, w_hbm, gain_ref, out_ref,
     w, gathered, resid, normed, hid_out, hid_in, slope, operand, total,
     part_out, part_in, done,
-    w_sem, hid_send, hid_recv, part_send, part_recv, row_send, row_recv, res_send, res_recv,
+    w_sem, hid_send, hid_recv, part_send, part_recv, row_send, row_recv, pass_send, res_send, res_recv,
 ):
     stride = 2 * stacks
     share, width = x_ref.shape[1], x_ref.shape[2]
@@ -220,6 +219,7 @@
     stack = (s % stride) // 2
     is_down = s % 2
     is_up = is_down == 0
+    sibling = t + 1 - 2 * (t % 2)
     first = layer == 0
     last = layer == LAYERS - 1
     peer = s + 1 - 2 * is_down
@@ -257,6 +257,15 @@
             device_id=(section, j), device_id_type=MESH,
         )
 
+    def pass_copy(m, i):
+        return pltpu.make_async_remote_copy(
+            gathered.at[m, i], gathered.at[m, i], pass_send.at[m, i], row_recv.at[m, i],
+            device_id=(s, sibling), device_id_type=MESH,
+        )
+
+    def row_wait(m, i):
+        pltpu.make_async_copy(gathered.at[m, i], gathered.at[m, i], row_recv.at[m, i]).wait()
+
     def res_copy(m):
         return pltpu.make_async_remote_copy(
             done.at[m], resid.at[m], res_send.at[m], res_recv.at[m],
@@ -313,7 +322,7 @@
 
         @pl.when(entry)
         def _():
-            for d in range(1, tensors):
+            for d in range(2, tensors, 2):
                 row_copy(m, other(d), s).start()
             gathered[m, t] = done[m]
 
@@ -321,13 +330,16 @@
     sequences = orders(batches)
 
     def project(step, m):
-        for d in range(1, tensors):
-            j = other(d)
-            pltpu.make_async_copy(gathered.at[m, j], gathered.at[m, j], row_recv.at[m, j]).wait()
-
-        @pl.when(has_prev_rows)
-        def _():
-            pltpu.make_async_copy(gathered.at[m, t], gathered.at[m, t], row_recv.at[m, t]).wait()
+        @pl.when(has_next)
+        def _():
+            row_wait(m, t)
+
+        pass_copy(m, t).start()
+        for d in range(2, tensors, 2):
+            row_wait(m, other(d))
+            pass_copy(m, other(d)).start()
+        for d in range(0, tensors, 2):
+            row_wait(m, lax.rem(sibling + d, tensors))
 
         @pl.when(is_up)
         def _():
@@ -423,11 +435,9 @@
         @pl.when(has_next)
         def _():
             done[m] = out_ref[m]
-            for d in range(tensors):
+            for d in range(0, tensors, 2):
                 row_copy(m, other(d), target).start()
             res_copy(m).start()
-
-    has_prev_rows = ~entry
 
     def advance(step, carry):
         code = 0
@@ -466,8 +476,10 @@
         for d in range(1, tensors):
             part_copy(m, other(d)).wait_send()
 
-        for d in range(1, tensors):
+        for d in range(2, tensors, 2):
             row_copy(m, other(d), s).wait_send()
+        for d in range(0, tensors, 2):
+            pass_copy(m, other(d)).wait_send()
 
         @pl.when(has_next)
         def _():
@@ -483,8 +495,9 @@
     sections, tensors = mesh_shape["section"], mesh_shape["tensor"]
     stacks = sections // (2 * LAYERS)
     width, hidden = weights.shape[1], weights.shape[2]
-    batches = inputs.shape[0] // stacks
-    share = inputs.shape[1] // width
+    split = inputs.shape[1] // (ROW_TILE * width)
+    batches = inputs.shape[0] // stacks * split
+    share = inputs.shape[1] // (width * split)
     rows = share * tensors
     piece = chunk_of(width, hidden)
     chunks = hidden // piece
@@ -516,6 +529,7 @@
             dma((batches, tensors)),
             dma((batches, tensors)),
             dma((batches, tensors)),
+            dma((batches, tensors)),
             dma((batches,)),
             dma((batches,)),
         ],
@@ -528,7 +542,7 @@
         weights[0],
         norm_gains,
     )
-    return out.reshape(1, batches, share * width)
+    return out.reshape(1, batches // split, split * share * width)
 
 
 def chunk_of(width, hidden):
@@ -545,7 +559,7 @@
         tensors = mesh.shape["tensor"]
         width, hidden = weights.shape[1], weights.shape[2] // tensors
         local = inputs.shape[1] // tensors
-        aligned = local % (ROW_TILE * width) == 0 and chunk_of(width, hidden)
+        aligned = local % (ROW_TILE * width) == 0 and tensors % 2 == 0 and chunk_of(width, hidden)
         body = functools.partial(relay_body, dict(mesh.shape)) if aligned else plain_body
         return jax.shard_map(
             body, mesh=mesh, in_specs=placed, out_specs=P("section", None, "tensor"), check_vma=False

time: 188 us -> 166 us (0.88)
  Pallas kernels: 184 us -> 160 us
    pallas_call x1, Pallas kernels: 184 us -> 160 us  [relay_body(): pl.pallas_call(functools.partial(relay_kernel, sections, tensors, stacks,...]
where the time goes in v2:
time: 166 us; the launch traced here: 165 us
  Pallas kernels  160 us (96%)
  local copies, waits for them, and re-layouts  5.07 us (3%)
    pallas_call x1, Pallas kernels, relay_body(): pl.pallas_call(functools.partial(relay_kernel, sections, tensors, stacks,...  160 us

profile of v2, /device:TPU:0, one launch (start us, length us, event | category | flops | bytes accessed | tf_op | source)
XLA Modules:
  0.0 165.4 jit_solution(18150676128451250245)
XLA Ops:
  0.0 1.7 %reshape.9.x_ref = bf16[4,8,2560]{2,1,0:T(8,128)(2,1)} reshape(bf16[2,40960]{1,0:T(2,128)(2,1)} %param.4) | data formatting | bytes 327680 | tf_op jit(solution)/shard_map/reshape | solution.py:540
  1.7 1.7 %reshape.10.g_ref = bf16[4,8,2560]{2,1,0:T(8,128)(2,1)} reshape(bf16[2,40960]{1,0:T(2,128)(2,1)} %param.5) | data formatting | bytes 327680 | tf_op jit(solution)/shard_map/reshape | solution.py:541
  3.4 160.3 %shard_map.46 = bf16[4,8,2560]{2,1,0:T(8,128)(2,1)} custom-call(bf16[4,8,2560]{2,1,0:T(8,128)(2,1)} %reshape.9.x_ref, bf16[4,8,2560]{2,1,0:T(8,128)(2,1)} %reshape.10.g_ref, bf16[2560,2560]{1,0:T(8,128)(2,1)} %bitcast.1, f32[4,2560]{1,0:T(4,128)} %gain_ref.1), custom_call_target="tpu_custom_call" | custom-call | tf_op jit(solution)/shard_map/pallas_call | solution.py:507
  163.7 1.7 %reshape.11 = bf16[1,2,40960]{2,1,0:T(2,128)(2,1)} reshape(bf16[4,8,2560]{2,1,0:T(8,128)(2,1)} %shard_map.46) | data formatting | bytes 327680 | tf_op jit(solution)/shard_map/reshape | solution.py:545

commit v3 on v2

--- a/solution.py
+++ b/solution.py
@@ -185,7 +185,7 @@
 ROW_TILE = 8
 GELU_C = 0.7978845608028654
 GELU_A = 0.044715
-PROJECT, COLLECT, FINISH = range(3)
+PROJECT, COLLECT, FINISH, FLIP = range(4)
 
 
 def orders(batches):
@@ -199,13 +199,14 @@
                 order += [FINISH * batches + m - 1]
     back += [FINISH * batches + batches - 1]
     turn += [FINISH * batches + batches - 1]
-    return project + back, turn, back + project, project + back
+    flip = [FLIP * batches]
+    return project + flip + back, flip + turn, flip + back + project, flip + project + back
 
 
 def relay_kernel(
     sections, tensors, stacks, batches,
     x_ref, g_ref, w_hbm, gain_ref, out_ref,
-    w, gathered, resid, normed, hid_out, hid_in, slope, operand, total,
+    w, flipped, gathered, resid, normed, hid_out, hid_in, slope, operand, total,
     part_out, part_in, done,
     w_sem, hid_send, hid_recv, part_send, part_recv, row_send, row_recv, pass_send, res_send, res_recv,
 ):
@@ -378,14 +379,25 @@
 
         lax.fori_loop(0, chunks, one, 0)
 
-    def collect(step, m):
-        total[...] = jnp.zeros_like(total)
-
+    def flip(step):
         def one(c, carry):
             @pl.when(step == 0)
             def _():
                 weight_copy(c).wait()
 
+            def block(n, inner):
+                at = pl.ds(pl.multiple_of(n * piece, piece), piece)
+                flipped[c, :, at] = w[c, at, :].T
+                return inner
+
+            return lax.fori_loop(0, width // piece, block, carry)
+
+        lax.fori_loop(0, chunks, one, 0)
+
+    def collect(m):
+        total[...] = jnp.zeros_like(total)
+
+        def one(c, carry):
             hid_copy(m, c).wait_recv()
 
             @pl.when(is_up)
@@ -398,7 +410,9 @@
 
             for n in range(width // piece):
                 cut = slice(n * piece, (n + 1) * piece)
-                total[:, cut] += project_back(operand[...], w[c, cut, :])
+                total[:, cut] += jnp.dot(
+                    operand[...], flipped[c, :, cut], preferred_element_type=jnp.float32
+                )
             return carry
 
         lax.fori_loop(0, chunks, one, 0)
@@ -441,7 +455,7 @@
 
     def advance(step, carry):
         code = 0
-        for i in range(3 * batches):
+        for i in range(len(sequences[0])):
             steady_up, last_up, steady_down, last_down = (table[i] for table in sequences)
             chosen = jnp.where(
                 is_up,
@@ -457,7 +471,11 @@
 
         @pl.when(kind == COLLECT)
         def _():
-            collect(step, m)
+            collect(m)
+
+        @pl.when(kind == FLIP)
+        def _():
+            flip(step)
 
         @pl.when(kind == FINISH)
         def _():
@@ -465,7 +483,7 @@
 
         return carry
 
-    lax.fori_loop(0, 3 * batches, advance, 0)
+    lax.fori_loop(0, len(sequences[0]), advance, 0)
 
     def drain(m, carry):
         def drain_hidden(c, inner):
@@ -511,6 +529,7 @@
         out_specs=vmem,
         scratch_shapes=[
             pltpu.VMEM((chunks, width, piece), bf16),
+            pltpu.VMEM((chunks, piece, width), bf16),
             pltpu.VMEM((batches, tensors, share, width), bf16),
             pltpu.VMEM((batches, share, width), bf16),
             pltpu.VMEM((rows, width), bf16),

time: 166 us -> 150 us (0.904)
  Pallas kernels: 160 us -> 144 us
    pallas_call x1, Pallas kernels: 160 us -> 144 us  [relay_body(): pl.pallas_call(functools.partial(relay_kernel, sections, tensors, stacks,...]
where the time goes in v3:
time: 150 us; the launch traced here: 149 us
  Pallas kernels  144 us (96%)
  local copies, waits for them, and re-layouts  5.07 us (3%)
    pallas_call x1, Pallas kernels, relay_body(): pl.pallas_call(functools.partial(relay_kernel, sections, tensors, stacks,...  144 us

profile of v3, /device:TPU:0, one launch (start us, length us, event | category | flops | bytes accessed | tf_op | source)
XLA Modules:
  0.0 149.5 jit_solution(5994221110279046663)
XLA Ops:
  0.0 1.7 %reshape.9.x_ref = bf16[4,8,2560]{2,1,0:T(8,128)(2,1)} reshape(bf16[2,40960]{1,0:T(2,128)(2,1)} %param.4) | data formatting | bytes 327680 | tf_op jit(solution)/shard_map/reshape | solution.py:559
  1.7 1.7 %reshape.10.g_ref = bf16[4,8,2560]{2,1,0:T(8,128)(2,1)} reshape(bf16[2,40960]{1,0:T(2,128)(2,1)} %param.5) | data formatting | bytes 327680 | tf_op jit(solution)/shard_map/reshape | solution.py:560
  3.4 144.4 %shard_map.46 = bf16[4,8,2560]{2,1,0:T(8,128)(2,1)} custom-call(bf16[4,8,2560]{2,1,0:T(8,128)(2,1)} %reshape.9.x_ref, bf16[4,8,2560]{2,1,0:T(8,128)(2,1)} %reshape.10.g_ref, bf16[2560,2560]{1,0:T(8,128)(2,1)} %bitcast.1, f32[4,2560]{1,0:T(4,128)} %gain_ref.1), custom_call_target="tpu_custom_call" | custom-call | tf_op jit(solution)/shard_map/pallas_call | solution.py:525
  147.8 1.7 %reshape.11 = bf16[1,2,40960]{2,1,0:T(2,128)(2,1)} reshape(bf16[4,8,2560]{2,1,0:T(8,128)(2,1)} %shard_map.46) | data formatting | bytes 327680 | tf_op jit(solution)/shard_map/reshape | solution.py:564
